TPU v7x, 32 devices: a whole 2x2x4 slice. The times are simulated.
32 devices in a mesh: groups: 2 (over y), branch: 4 (over z), leaf: 4 (over x, core).
Axes of the slice: x: 2, y: 2, z: 4, core: 2. Of those that a mesh axis runs over, the one named last changes fastest.
Arguments:
- queries: float32 [4096, 1024], P(('groups', 'branch', 'leaf')), parts along dimension 0, may hold values from -32 to 32
- leaf_keys: float32 [4096, 128], P(('groups', 'branch', 'leaf')), parts along dimension 0, may hold values from -6 to 6
- leaf_values: float32 [4096, 128], P(('groups', 'branch', 'leaf')), parts along dimension 0, may hold values from -6 to 6
- root_keys: float32 [512, 128], P(('groups', 'branch', 'leaf')), parts along dimension 0, may hold values from -12 to 12
- root_values: float32 [512, 128], P(('groups', 'branch', 'leaf')), parts along dimension 0, may hold values from -6 to 6
- branch_keys: float32 [2048, 128], P(('groups', 'branch', 'leaf')), parts along dimension 0, may hold values from -6 to 6
- branch_values: float32 [2048, 128], P(('groups', 'branch', 'leaf')), parts along dimension 0, may hold values from -6 to 6
- d_out: float32 [4096, 1024], P(('groups', 'branch', 'leaf')), parts along dimension 0, may hold values from -6 to 6
- leaf_len: int32 [32], P(('groups', 'branch', 'leaf')), parts along dimension 0, may hold values from 1 to 128, 1280 in all
- leaf_parent: int32 [32], P(('groups', 'branch', 'leaf')), parts along dimension 0, may hold values from 0 to 255
- root_cut: int32 [8], P(('groups', 'branch')), parts along dimension 0, may hold values from 128 to 256
Outputs:
- attended: float32 [4096, 1024], P(('groups', 'branch', 'leaf')), parts along dimension 0
- d_queries: float32 [4096, 1024], P(('groups', 'branch', 'leaf')), parts along dimension 0
- d_root_kv: float32 [512, 256], P(('groups', 'branch', 'leaf')), parts along dimension 0
- d_branch_kv: float32 [2048, 256], P(('groups', 'branch', 'leaf')), parts along dimension 0
- d_leaf_kv: float32 [4096, 256], P(('groups', 'branch', 'leaf')), parts along dimension 0
There are 2 independent parts, one for each index of `groups`. A program takes and returns all parts, laid end to end along the dimension named above; each array names one. Nothing has to cross between parts.
Inputs may be any that keep to these rules, and one draw needn't show every extreme that they name: `leaf_len`: the lengths of one tree sum to 1280, and some leaf holds 128 live tokens.
All inputs are finite; a program needn't handle non-finite values. No bound on the sum of `leaf_len` on one device may be relied on, other than what follows from the above.
Results may differ from a plain program's by a relative error of at most 0.0003.
Values sent between devices are 32-bit elements; how exact they have to be, the bound alone decides.
A program may use at most 64 MiB of HBM per device.

v0:
```python
import math

import jax
import jax.numpy as jnp
from jax import lax
from jax.sharding import PartitionSpec as P

key_block = 256


def shards(
    queries,
    leaf_keys,
    leaf_values,
    root_keys,
    root_values,
    branch_keys,
    branch_values,
    d_out,
    leaf_len,
    leaf_parent,
    root_cut,
):
    row_count, row_width = queries.shape
    head_dim = leaf_keys.shape[1]
    head_count = row_width // head_dim
    score_scale = 1.0 / math.sqrt(head_dim)
    highest = lax.Precision.HIGHEST
    whole_root_keys, whole_root_values = (
        lax.all_gather(root_keys, ("branch", "leaf"), axis=0, tiled=True),
        lax.all_gather(root_values, ("branch", "leaf"), axis=0, tiled=True),
    )
    slice_keys, slice_values = (
        lax.all_gather(branch_keys, "leaf", axis=0, tiled=True),
        lax.all_gather(branch_values, "leaf", axis=0, tiled=True),
    )
    root_count = whole_root_keys.shape[0]
    slice_count = slice_keys.shape[0]
    key_count = root_count + slice_count + row_count
    block_count = -(-key_count // key_block)
    padding = block_count * key_block - key_count
    filler = jnp.zeros((padding, head_dim), jnp.float32)
    all_keys = jnp.concatenate([whole_root_keys, slice_keys, leaf_keys, filler], axis=0).reshape(
        block_count, key_block, head_dim
    )
    all_values = jnp.concatenate(
        [whole_root_values, slice_values, leaf_values, filler], axis=0
    ).reshape(block_count, key_block, head_dim)
    query_heads = queries.reshape(row_count, head_count, head_dim)
    positions = jnp.arange(row_count, dtype=jnp.int32)[:, None]
    root_limit = root_cut[0]
    parent = leaf_parent[0]
    length = leaf_len[0]
    live_rows = (positions[:, 0] < length).astype(jnp.float32)[:, None, None]

    def masked_scores(block_index, block_keys):
        columns = block_index * key_block + jnp.arange(key_block, dtype=jnp.int32)[None, :]
        in_root = columns < root_limit
        in_slice = (
            (columns >= root_count)
            & (columns < root_count + slice_count)
            & (columns - root_count <= parent)
        )
        in_leaf = (columns >= root_count + slice_count) & (
            columns - root_count - slice_count <= positions
        )
        visible = in_root | in_slice | in_leaf
        scores = jnp.einsum("thd,kd->thk", query_heads, block_keys, precision=highest) * score_scale
        return jnp.where(visible[:, None, :], scores, -jnp.inf)

    def forward_step(running, inputs):
        running_max, running_sum, running_acc = running
        block_index, block_keys, block_values = inputs
        scores = masked_scores(block_index, block_keys)
        new_max = jnp.maximum(running_max, jnp.max(scores, axis=-1))
        raised = jnp.exp(scores - new_max[..., None])
        factor = jnp.exp(running_max - new_max)
        running_sum = running_sum * factor + jnp.sum(raised, axis=-1)
        running_acc = running_acc * factor[..., None] + jnp.einsum(
            "thk,kd->thd", raised, block_values, precision=highest
        )
        return ((new_max, running_sum, running_acc), None)

    block_ids = jnp.arange(block_count, dtype=jnp.int32)
    initial = (
        jnp.full((row_count, head_count), -jnp.inf, jnp.float32),
        jnp.zeros((row_count, head_count), jnp.float32),
        jnp.zeros((row_count, head_count, head_dim), jnp.float32),
    )
    finals, unused = lax.scan(forward_step, initial, (block_ids, all_keys, all_values))
    run_max, run_sum, run_acc = finals
    unmasked = run_acc / run_sum[..., None]
    log_total = run_max + jnp.log(run_sum)
    attended = (unmasked * live_rows).reshape(row_count, row_width)
    cotangent = d_out.reshape(row_count, head_count, head_dim) * live_rows
    row_dot = jnp.sum(cotangent * unmasked, axis=-1)

    def backward_step(query_grad, inputs):
        block_index, block_keys, block_values = inputs
        weights = jnp.exp(masked_scores(block_index, block_keys) - log_total[..., None])
        weight_grad = jnp.einsum("thd,kd->thk", cotangent, block_values, precision=highest)
        score_grad = weights * (weight_grad - row_dot[..., None]) * score_scale
        query_grad = query_grad + jnp.einsum(
            "thk,kd->thd", score_grad, block_keys, precision=highest
        )
        key_grad = jnp.einsum("thk,thd->kd", score_grad, query_heads, precision=highest)
        value_grad = jnp.einsum("thk,thd->kd", weights, cotangent, precision=highest)
        return (query_grad, jnp.concatenate([key_grad, value_grad], axis=1))

    query_grad, pair_blocks = lax.scan(
        backward_step, jnp.zeros_like(query_heads), (block_ids, all_keys, all_values)
    )
    pair_rows = pair_blocks.reshape(block_count * key_block, 2 * head_dim)
    root_term = pair_rows[:root_count]
    slice_term = pair_rows[root_count : root_count + slice_count]
    leaf_pairs = pair_rows[root_count + slice_count : key_count]
    partial_root = lax.psum_scatter(root_term, "branch", scatter_dimension=0, tiled=True)
    root_gradient, slice_gradient = (
        lax.psum_scatter(partial_root, "leaf", scatter_dimension=0, tiled=True),
        lax.psum_scatter(slice_term, "leaf", scatter_dimension=0, tiled=True),
    )
    return (
        attended,
        query_grad.reshape(row_count, row_width),
        root_gradient,
        slice_gradient,
        leaf_pairs,
    )


def solution(mesh):
    in_specs = (
        P(("groups", "branch", "leaf"), None),
        P(("groups", "branch", "leaf"), None),
        P(("groups", "branch", "leaf"), None),
        P(("groups", "branch", "leaf"), None),
        P(("groups", "branch", "leaf"), None),
        P(("groups", "branch", "leaf"), None),
        P(("groups", "branch", "leaf"), None),
        P(("groups", "branch", "leaf"), None),
        P(("groups", "branch", "leaf")),
        P(("groups", "branch", "leaf")),
        P(("groups", "branch")),
    )
    out_specs = (
        P(("groups", "branch", "leaf"), None),
        P(("groups", "branch", "leaf"), None),
        P(("groups", "branch", "leaf"), None),
        P(("groups", "branch", "leaf"), None),
        P(("groups", "branch", "leaf"), None),
    )
    return jax.shard_map(shards, mesh=mesh, in_specs=in_specs, out_specs=out_specs, check_vma=False)
```

profile of v0, /device:TPU:0, one launch (start us, length us, event | category | flops | bytes accessed | tf_op | source)
XLA Modules:
  0.0 188.2 jit_solution(6217070685532324727)
XLA Ops:
  8.0 25.1 %all_gather.12 = f32[256,128]{1,0:T(8,128)} all-gather(f32[16,128]{1,0:T(8,128)} %param.18), channel_id=1, replica_groups=mesh['groups'=2,'branch'=4,'leaf'=4] {'branch','leaf'}, dimensions={0}, use_global_device_ids=true | all-gather | bytes 139264 | tf_op jit(solution)/shard_map/all_gather | solution.py:30
  33.1 19.4 %all_gather.14 = f32[256,128]{1,0:T(8,128)} all-gather(f32[16,128]{1,0:T(8,128)} %param.19), channel_id=1, replica_groups=mesh['groups'=2,'branch'=4,'leaf'=4] {'branch','leaf'}, dimensions={0}, use_global_device_ids=true | all-gather | bytes 139264 | tf_op jit(solution)/shard_map/all_gather | solution.py:31
  52.5 5.6 %all_gather.13 = f32[256,128]{1,0:T(8,128)S(1)} all-gather(f32[64,128]{1,0:T(8,128)} %param.20), channel_id=1, replica_groups=mesh['groups'=2,'branch'=4,'leaf'=4] {'leaf'}, dimensions={0}, use_global_device_ids=true | all-gather | bytes 163840 | tf_op jit(solution)/shard_map/all_gather | solution.py:34
  58.1 7.1 %all_gather.15 = f32[256,128]{1,0:T(8,128)} all-gather(f32[64,128]{1,0:T(8,128)} %param.21), channel_id=1, replica_groups=mesh['groups'=2,'branch'=4,'leaf'=4] {'leaf'}, dimensions={0}, use_global_device_ids=true | all-gather | bytes 163840 | tf_op jit(solution)/shard_map/all_gather | solution.py:35
  65.6 0.8 copy-done.1
  66.6 1.3 maximum_maximum_fusion.1
  67.9 17.9 %while.38 = (s32[]{:T(128)}, f32[128,8]{0,1:T(8,128)S(1)}, f32[128,8]{0,1:T(8,128)S(1)}, f32[128,8,128]{2,0,1:T(8,128)S(1)}, s32[3]{0:T(128)S(1)}, /*index=5*/s3...) while((s32[]{:T(128)}, f32[128,8]{0,1:T(8,128)S(1)}, ...), condition=%wide.region_3.4_spmd.clone, body=%wide.region_0.3_spmd.clone.sunk | while | flops 807378944 | bytes 5115073 | solution.py:90
  69.2 1.3 and_or_fusion.4
  70.6 1.1 fusion.74
  71.9 1.9 %convolution_add_fusion.4 = f32[128,8,128]{2,0,1:T(8,128)S(1)} fusion(f32[128,8,256]{0,2,1:T(8,128)S(1)} %get-tuple-element.823, f32[128,8,128]{2,0,1:T(8,128)S(1)} %get-tuple-element.856, f32[128,8]{0,1:T(8,128)S(1)} %select_maximum_fusion.2, f32[128,8]{0,1:T(8,128)S(1)} %get-tuple-element.825, pred[]{:T(512)S(6)} %compare.6, ...), kind=kOutput, calls=%fused_computation.5.clone.1 | convolution fusion | flops 403308544 | bytes 2236421 | tf_op jit(solution)/shard_map/while/body/eval_jaxpr/thk,kd->thd/dot_general | solution.py:79
  75.1 1.3 and_or_fusion.4
  76.6 1.1 fusion.74
  77.9 1.9 %convolution_add_fusion.4 = f32[128,8,128]{2,0,1:T(8,128)S(1)} fusion(f32[128,8,256]{0,2,1:T(8,128)S(1)} %get-tuple-element.823, f32[128,8,128]{2,0,1:T(8,128)S(1)} %get-tuple-element.856, f32[128,8]{0,1:T(8,128)S(1)} %select_maximum_fusion.2, f32[128,8]{0,1:T(8,128)S(1)} %get-tuple-element.825, pred[]{:T(512)S(6)} %compare.6, ...), kind=kOutput, calls=%fused_computation.5.clone.1 | convolution fusion | flops 403308544 | bytes 2236421 | tf_op jit(solution)/shard_map/while/body/eval_jaxpr/thk,kd->thd/dot_general | solution.py:79
  81.1 1.3 and_or_fusion.4
  82.6 1.0 fusion.74
  83.8 1.9 %convolution_add_fusion.4 = f32[128,8,128]{2,0,1:T(8,128)S(1)} fusion(f32[128,8,256]{0,2,1:T(8,128)S(1)} %get-tuple-element.823, f32[128,8,128]{2,0,1:T(8,128)S(1)} %get-tuple-element.856, f32[128,8]{0,1:T(8,128)S(1)} %select_maximum_fusion.2, f32[128,8]{0,1:T(8,128)S(1)} %get-tuple-element.825, pred[]{:T(512)S(6)} %compare.6, ...), kind=kOutput, calls=%fused_computation.5.clone.1 | convolution fusion | flops 403308544 | bytes 2236421 | tf_op jit(solution)/shard_map/while/body/eval_jaxpr/thk,kd->thd/dot_general | solution.py:79
  85.8 1.0 copy.24
  86.8 1.2 multiply_reduce_fusion
  88.0 30.4 %while.39 = (s32[]{:T(128)}, f32[128,8,128]{2,0,1:T(8,128)S(1)}, f32[3,256,256]{2,1,0:T(8,128)}, s32[3]{0:T(128)S(1)}, s32[]{:T(128)}, /*index=5*/s32[]{:T(128)}...) while((s32[]{:T(128)}, f32[128,8,128]{2,0,1:T(8,128)S(1)}, ...), condition=%wide.region_6.7_spmd.clone, body=%wide.region_5.6_spmd.clone.sunk | while | flops 2015267840 | bytes 11742423 | solution.py:110
  89.2 1.3 and_or_fusion.5
  90.7 1.1 fusion.89
  91.8 1.2 convolution_bitcast_fusion.4
  93.0 1.0 fusion.90
  94.1 1.2 convolution_bitcast_fusion.5
  95.3 2.0 %convolution_add_fusion.5 = f32[128,8,128]{2,0,1:T(8,128)S(1)} fusion(f32[128,8,256]{0,2,1:T(8,128)S(1)} %fusion.90, f32[128,8,128]{2,0,1:T(8,128)S(1)} %get-tuple-element.895, pred[]{:T(512)S(6)} %compare.7, f32[3,256,128]{2,1,0:T(8,128)S(1)} %get-tuple-element.915, s32[]{:T(128)S(6)} %copy.61), kind=kOutput, calls=%fused_computation.36.clone.1 | convolution fusion | flops 402915328 | bytes 2228229 | tf_op jit(solution)/shard_map/while/body/eval_jaxpr/thk,kd->thd/dot_general | solution.py:103
  97.4 0.7 constant_dynamic-update-slice_fusion.2
  99.3 1.3 and_or_fusion.5
  100.8 1.1 fusion.89
  102.0 1.2 convolution_bitcast_fusion.4
  103.1 1.0 fusion.90
  104.2 1.2 convolution_bitcast_fusion.5
  105.4 2.0 %convolution_add_fusion.5 = f32[128,8,128]{2,0,1:T(8,128)S(1)} fusion(f32[128,8,256]{0,2,1:T(8,128)S(1)} %fusion.90, f32[128,8,128]{2,0,1:T(8,128)S(1)} %get-tuple-element.895, pred[]{:T(512)S(6)} %compare.7, f32[3,256,128]{2,1,0:T(8,128)S(1)} %get-tuple-element.915, s32[]{:T(128)S(6)} %copy.61), kind=kOutput, calls=%fused_computation.36.clone.1 | convolution fusion | flops 402915328 | bytes 2228229 | tf_op jit(solution)/shard_map/while/body/eval_jaxpr/thk,kd->thd/dot_general | solution.py:103
  107.5 0.7 constant_dynamic-update-slice_fusion.2
  109.5 1.3 and_or_fusion.5
  111.0 1.1 fusion.89
  112.1 1.2 convolution_bitcast_fusion.4
  113.3 1.0 fusion.90
  114.3 1.2 convolution_bitcast_fusion.5
  115.5 2.0 %convolution_add_fusion.5 = f32[128,8,128]{2,0,1:T(8,128)S(1)} fusion(f32[128,8,256]{0,2,1:T(8,128)S(1)} %fusion.90, f32[128,8,128]{2,0,1:T(8,128)S(1)} %get-tuple-element.895, pred[]{:T(512)S(6)} %compare.7, f32[3,256,128]{2,1,0:T(8,128)S(1)} %get-tuple-element.915, s32[]{:T(128)S(6)} %copy.61), kind=kOutput, calls=%fused_computation.36.clone.1 | convolution fusion | flops 402915328 | bytes 2228229 | tf_op jit(solution)/shard_map/while/body/eval_jaxpr/thk,kd->thd/dot_general | solution.py:103
  117.6 0.7 constant_dynamic-update-slice_fusion.2
  118.3 1.9 slice_bitcast_fusion
  120.3 0.7 reduce-scatter.8.cloned.1.call-update
  121.0 1.0 copy.37
  122.0 1.6 slice.20
  123.6 14.2 %reduce-scatter.4.cloned.1.call-done = f32[64,256]{1,0:T(8,128)} async-done(((f32[256,256]{1,0:T(8,128)}), f32[64,256]{1,0:T(8,128)}) %reduce-scatter.4.cloned.1.call-update) | async-done | bytes 65552 | tf_op jit(solution)/shard_map/reduce_scatter | solution.py:117
  137.8 0.8 copy_bitcast_fusion
  138.6 20.5 %reduce-scatter.8.cloned.1.call-done = f32[64,256]{1,0:T(8,128)} async-done(((f32[256,256]{1,0:T(8,128)}), f32[64,256]{1,0:T(8,128)}) %reduce-scatter.8.cloned.1.call-update) | async-done | bytes 65552 | tf_op jit(solution)/shard_map/reduce_scatter | solution.py:120
  159.1 22.6 %reduce-scatter.6.cloned.1.call-done = f32[16,256]{1,0:T(8,128)} async-done(((f32[64,256]{1,0:T(8,128)}), f32[16,256]{1,0:T(8,128)}) %reduce-scatter.6.cloned.1.call-update) | async-done | bytes 16400 | tf_op jit(solution)/shard_map/reduce_scatter | solution.py:119
  (58 shorter events, 6.3 us)
Async XLA Ops:
  7.2 58.0 %copy-start = (f32[128,1024]{1,0:T(8,128)S(1)}, f32[128,1024]{1,0:T(8,128)}, u32[]{:S(2)}) copy-start(f32[128,1024]{1,0:T(8,128)} %param.15) | copy-start | bytes 1572868
  7.2 130.6 %reduce-scatter.4.cloned.1.call-start = ((), (), s32[]{:S(2)}) async-start(), calls=%async_computation.3 | async-start | bytes 327680 | tf_op jit(solution)/shard_map/reduce_scatter | solution.py:117
  65.3 1.0 copy-start.1
  120.2 38.9 %reduce-scatter.8.cloned.1.call-start = ((), (), s32[]{:S(2)}) async-start(), calls=%async_computation.5 | async-start | bytes 327680 | tf_op jit(solution)/shard_map/reduce_scatter | solution.py:120
  121.0 60.7 %reduce-scatter.6.cloned.1.call-start = ((), (), s32[]{:S(2)}) async-start(), calls=%async_computation.4 | async-start | bytes 81920 | tf_op jit(solution)/shard_map/reduce_scatter | solution.py:119
Sparse Core Ops, SparseCore 0:
  120.3 17.3 reduce-scatter.3
  140.8 18.2 reduce-scatter.7
  162.1 19.5 reduce-scatter.5
where the time goes:
time: 189 us; the launch traced here: 188 us
  waiting for transfers between devices  57.9 us (31%)
  blocking collectives  57.2 us (30%)
  matrix products  28.4 us (15%)
  between operations  14.6 us (8%)
  local copies, waits for them, and re-layouts  13.7 us (7%)
  other arithmetic  11.9 us (6%)
  loops' own time  4.39 us (2%)
    all_gather x1, blocking collectives, shards(): lax.all_gather(root_keys, ('branch', 'leaf'), axis=0, tiled=True)  25.1 us
    reduce_scatter x1, waiting for transfers between devices, shards(): lax.psum_scatter(partial_root, 'leaf', scatter_dimension=0, tiled=True)  22.6 us
    reduce_scatter x1, waiting for transfers between devices, shards(): lax.psum_scatter(slice_term, 'leaf', scatter_dimension=0, tiled=True)  20.5 us
    all_gather x1, blocking collectives, shards(): lax.all_gather(root_values, ('branch', 'leaf'), axis=0, tiled=True)  19.4 us
    reduce_scatter x1, waiting for transfers between devices, shards(): lax.psum_scatter(root_term, 'branch', scatter_dimension=0, tiled=True)  14.2 us
    or x12, other arithmetic, masked_scores(): visible = in_root | in_slice | in_leaf  8.83 us
    all_gather x1, blocking collectives, shards(): lax.all_gather(branch_values, 'leaf', axis=0, tiled=True)  7.05 us
    dot_general x6, matrix products, masked_scores(): jnp.einsum('thd,kd->thk', query_heads, block_keys, precision=highest)  6.5 us
  transfers between devices with their start and end apart: 3, of which 3 were waited for; matrix products, arithmetic and copies ran while one was open for 2% of the time, Pallas kernels for 0%

commit v1 on v0

v1 whole, which is shorter than its diff:
```python
import functools
import math

import jax
import jax.numpy as jnp
from jax import lax
from jax.experimental import pallas as pl
from jax.experimental.pallas import tpu as pltpu
from jax.sharding import PartitionSpec as P

f32 = jnp.float32
bf16 = jnp.bfloat16
hidden = -1e30


def split2(x):
    high = x.astype(bf16)
    return high, (x - high.astype(f32)).astype(bf16)


def split3(x):
    high = x.astype(bf16)
    rest = x - high.astype(f32)
    middle = rest.astype(bf16)
    return high, middle, (rest - middle.astype(f32)).astype(bf16)


def mm(a, b):
    return lax.dot_general(a, b, (((1,), (0,)), ((), ())), preferred_element_type=f32)


def mmt(a, b):
    return lax.dot_general(a, b, (((1,), (1,)), ((), ())), preferred_element_type=f32)


def side(*parts):
    return jnp.concatenate(parts, axis=1)


def kernel(
    nb, nx, nc, dims,
    q_hbm, lk_hbm, lv_hbm, rk_hbm, rv_hbm, bk_hbm, bv_hbm, do_hbm, len_ref, par_ref, cut_ref,
    att_hbm, dq_hbm, droot_ref, dslice_ref, dleaf_ref,
    q_ref, do_ref, leaf_ref, rootb, sliceb,
    qs, cs, ks, vs, kt, vt, sc, dp, dkv,
    att_ref, dqv_ref,
    rc_root, rc_slice, sn_root, sn_slice, rv_root, rv_slice,
    ld_sem, st_sem, gs_root, gr_root, gs_slice, gr_slice, cs_sem, cr_sem,
    ss_root, sr_root, ss_slice, sr_slice, es_sem, er_sem,
):
    T, H, D, r_rows, b_rows = dims
    R = T * H
    n_root = nb * nx * nc * r_rows
    n_slice = nx * nc * b_rows
    n_keys = n_root + n_slice + T
    scale = 1.0 / math.sqrt(D)
    g = lax.axis_index("groups")
    b = lax.axis_index("branch")
    leaf = lax.axis_index("leaf")
    x = leaf // nc
    c = leaf % nc
    pair = 2 * T if H % 2 == 0 else T
    per = pair // T
    n_pair = R // pair

    def dev(bb, xx, cc):
        return (g, bb, xx * nc + cc)

    def shifted(sb, sx):
        return lax.rem(b + sb, nb), lax.rem(x + sx, nx)

    peers = [(sb, sx) for sb in range(nb) for sx in range(nx) if sb or sx]
    other = lax.rem(c + 1, nc)

    loads = [
        (rk_hbm, rootb.at[b, x, c, 0]),
        (rv_hbm, rootb.at[b, x, c, 1]),
        (bk_hbm, sliceb.at[x, c, 0]),
        (bv_hbm, sliceb.at[x, c, 1]),
        (lk_hbm, leaf_ref.at[0]),
        (lv_hbm, leaf_ref.at[1]),
        (q_hbm, q_ref),
        (do_hbm, do_ref),
    ]
    loads = [pltpu.make_async_copy(s, d, ld_sem.at[i]) for i, (s, d) in enumerate(loads)]
    for cp in loads:
        cp.start()

    barrier = pltpu.get_barrier_semaphore()
    for sb, sx in peers:
        bb, xx = shifted(sb, sx)
        pl.semaphore_signal(barrier, inc=1, device_id=dev(bb, xx, c), device_id_type=pl.DeviceIdType.MESH)
    if nc == 2:
        pl.semaphore_signal(barrier, inc=1, device_id=dev(b, x, other), device_id_type=pl.DeviceIdType.MESH)
    pl.semaphore_wait(barrier, len(peers) + (nc == 2))

    def remote(src, dst, s_sem, r_sem, where):
        return pltpu.make_async_remote_copy(
            src_ref=src, dst_ref=dst, send_sem=s_sem, recv_sem=r_sem,
            device_id=where, device_id_type=pl.DeviceIdType.MESH,
        )

    for cp in loads[:4]:
        cp.wait()
    slice_sends, root_sends = [], []
    for sx in range(1, nx):
        bb, xx = shifted(0, sx)
        blk = sliceb.at[x, c]
        slice_sends.append(remote(blk, blk, gs_slice.at[sx], gr_slice.at[sx], dev(b, xx, c)))
    for i, (sb, sx) in enumerate(peers):
        bb, xx = shifted(sb, sx)
        blk = rootb.at[b, x, c]
        root_sends.append(remote(blk, blk, gs_root.at[i], gr_root.at[i], dev(bb, xx, c)))
    for cp in root_sends + slice_sends:
        cp.start()

    for cp in loads[4:]:
        cp.wait()
    live = lax.broadcasted_iota(jnp.int32, (T, D), 0) < len_ref[0]
    for h in range(H):
        cols = slice(h * D, (h + 1) * D)
        rows = slice(h * T, (h + 1) * T)
        q1, q2, q3 = split3(q_ref[:, cols])
        qs[0, rows], qs[1, rows], qs[2, rows] = q1, q2, q3
        c1, c2 = split2(jnp.where(live, do_ref[:, cols], 0.0))
        cs[0, rows], cs[1, rows] = c1, c2

    def stage(first, keys, values):
        count = keys.shape[0]
        span = slice(first, first + count)
        k1, k2, k3 = split3(keys)
        ks[span, :] = side(k1, k2, k3)
        v1, v2 = split2(values)
        vs[span, :] = side(v1, v2)
        ka, kb = split2(keys.T)
        kt[:D, span] = ka
        kt[D:, span] = kb
        va, vb = split2(values.T)
        vt[:D, span] = va
        vt[D:, span] = vb

    def score(first, count, seen):
        step = min(count, 256)

        def body(p, carry):
            rows = pl.ds(pl.multiple_of(p * pair, pair), pair)
            q1, q2, q3 = qs[0, rows, :], qs[1, rows, :], qs[2, rows, :]
            c1, c2 = cs[0, rows, :], cs[1, rows, :]
            qa, qb, qc = side(q1, q1), side(q2, q2), side(q3, q1)
            ca, cb = side(c1, c1), side(c2, c2)
            for lo in range(0, count, step):
                span = slice(first + lo, first + lo + step)
                k12 = ks[span, : 2 * D]
                k13 = side(ks[span, :D], ks[span, 2 * D :])
                s = mmt(k12, qa) + (mmt(k12, qb) + mmt(k13, qc))
                sc[span, rows] = jnp.where(seen(lo, step), s * scale, hidden)
                v12 = vs[span, :]
                dp[span, rows] = mmt(v12, ca) + mmt(v12, cb)
            return carry

        lax.fori_loop(0, n_pair, body, 0)

    def index_of(lo, step):
        return lo + lax.broadcasted_iota(jnp.int32, (step, pair), 0)

    def slot_of(step):
        return lax.broadcasted_iota(jnp.int32, (step, pair), 1) % T

    stage(n_root + n_slice, leaf_ref[0], leaf_ref[1])
    score(n_root + n_slice, T, lambda lo, step: index_of(lo, step) <= slot_of(step))

    core_sends = []
    for sx in range(1, nx):
        blk = sliceb.at[lax.rem(x + nx - sx, nx), c]
        remote(blk, blk, gs_slice.at[sx], gr_slice.at[sx], dev(b, x, c)).wait_recv()
    if nc == 2:
        cp = remote(sliceb.at[:, c], sliceb.at[:, c], cs_sem.at[0], cr_sem.at[0], dev(b, x, other))
        cp.start()
        core_sends.append(cp)
    for i, (sb, sx) in enumerate(peers):
        blk = rootb.at[lax.rem(b + nb - sb, nb), lax.rem(x + nx - sx, nx), c]
        remote(blk, blk, gs_root.at[i], gr_root.at[i], dev(b, x, c)).wait_recv()
    if nc == 2:
        cp = remote(rootb.at[:, :, c], rootb.at[:, :, c], cs_sem.at[1], cr_sem.at[1], dev(b, x, other))
        cp.start()
        core_sends.append(cp)
        remote(sliceb.at[:, other], sliceb.at[:, other], cs_sem.at[0], cr_sem.at[0], dev(b, x, other)).wait_recv()
    stage(
        n_root,
        sliceb[:, :, 0].reshape(n_slice, D),
        sliceb[:, :, 1].reshape(n_slice, D),
    )
    score(n_root, n_slice, lambda lo, step: index_of(lo, step) <= par_ref[0])
    if nc == 2:
        remote(rootb.at[:, :, other], rootb.at[:, :, other], cs_sem.at[1], cr_sem.at[1], dev(b, x, other)).wait_recv()
    stage(
        0,
        rootb[:, :, :, 0].reshape(n_root, D),
        rootb[:, :, :, 1].reshape(n_root, D),
    )
    score(0, n_root, lambda lo, step: index_of(lo, step) < cut_ref[0])

    chunk = 128

    def soften(p, carry):
        rows = pl.ds(pl.multiple_of(p * pair, pair), pair)
        spans = [slice(lo, lo + chunk) for lo in range(0, n_keys, chunk)]
        top = None
        for span in spans:
            m = jnp.max(sc[span, rows], axis=0, keepdims=True)
            top = m if top is None else jnp.maximum(top, m)
        total = jnp.zeros((1, pair), f32)
        dot = jnp.zeros((1, pair), f32)
        for span in spans:
            e = jnp.exp(sc[span, rows] - top)
            sc[span, rows] = e
            total = total + jnp.sum(e, axis=0, keepdims=True)
            dot = dot + jnp.sum(e * dp[span, rows], axis=0, keepdims=True)
        inverse = 1.0 / total
        dot = dot * inverse
        for span in spans:
            w = sc[span, rows] * inverse
            sc[span, rows] = w
            dp[span, rows] = w * (dp[span, rows] - dot) * scale
        return carry

    lax.fori_loop(0, n_pair, soften, 0)

    def key_gradients(first, step):
        span = pl.ds(first, step)
        s1, s2 = split2(dp[span, :])
        q12 = side(qs[0], qs[1])
        a = mm(s1, q12) + mm(s2, q12)
        w1, w2 = split2(sc[span, :])
        c12 = side(cs[0], cs[1])
        v = mm(w1, c12) + mm(w2, c12)
        return side(a[:, :D] + a[:, D:], v[:, :D] + v[:, D:])

    def gradient_block(i, carry):
        at = pl.multiple_of(i * chunk, chunk)
        dkv[pl.ds(at, chunk), :] = key_gradients(at, chunk)
        return carry

    root_g = dkv.at[:n_root].reshape(nb, nx, nc, r_rows, 2 * D)
    slice_g = dkv.at[n_root : n_root + n_slice].reshape(nx, nc, b_rows, 2 * D)
    lax.fori_loop(0, n_root // chunk, gradient_block, 0)
    ex = []
    if nc == 2:
        cp = remote(root_g.at[:, :, other], rc_root, es_sem.at[0], er_sem.at[0], dev(b, x, other))
        cp.start()
        ex.append(cp)
    lax.fori_loop(n_root // chunk, (n_root + n_slice) // chunk, gradient_block, 0)
    if nc == 2:
        cp = remote(slice_g.at[:, other], rc_slice, es_sem.at[1], er_sem.at[1], dev(b, x, other))
        cp.start()
        ex.append(cp)
        ex[0].wait_recv()
    mine = root_g[:, :, c]
    sn_root[...] = mine + rc_root[...] if nc == 2 else mine
    fin_root = []
    for i, (sb, sx) in enumerate(peers):
        bb, xx = shifted(sb, sx)
        fin_root.append(remote(sn_root.at[bb, xx], rv_root.at[i], ss_root.at[i], sr_root.at[i], dev(bb, xx, c)))
        fin_root[-1].start()
    if nc == 2:
        ex[1].wait_recv()
    mine = slice_g[:, c]
    sn_slice[...] = mine + rc_slice[...] if nc == 2 else mine
    fin_slice = []
    for sx in range(1, nx):
        bb, xx = shifted(0, sx)
        fin_slice.append(
            remote(sn_slice.at[xx], rv_slice.at[sx - 1], ss_slice.at[sx], sr_slice.at[sx], dev(b, xx, c))
        )
        fin_slice[-1].start()

    def outputs(p, carry):
        rows = pl.ds(pl.multiple_of(p * pair, pair), pair)
        w1, w2 = split2(sc[:, rows])
        m = mm(vt[...], w1) + mm(vt[...], w2)
        m = m[:D] + m[D:]
        s1, s2 = split2(dp[:, rows])
        n = mm(kt[...], s1) + mm(kt[...], s2)
        n = n[:D] + n[D:]
        for k in range(per):
            cols = pl.ds(pl.multiple_of(p * (per * D) + k * D, D), D)
            part = slice(k * T, (k + 1) * T)
            att_ref[:, cols] = jnp.where(live, m[:, part].T, 0.0)
            dqv_ref[:, cols] = n[:, part].T
        return carry

    lax.fori_loop(0, n_pair, outputs, 0)
    out_a = pltpu.make_async_copy(att_ref, att_hbm, st_sem.at[0])
    out_q = pltpu.make_async_copy(dqv_ref, dq_hbm, st_sem.at[1])
    out_a.start()
    out_q.start()
    dleaf_ref[...] = key_gradients(n_root + n_slice, T)

    for cp in fin_slice:
        cp.wait_recv()
    total = sn_slice[x]
    for i in range(nx - 1):
        total = total + rv_slice[i]
    dslice_ref[...] = total
    for cp in fin_root:
        cp.wait_recv()
    total = sn_root[b, x]
    for i in range(len(peers)):
        total = total + rv_root[i]
    droot_ref[...] = total
    for cp in root_sends + slice_sends + core_sends + ex + fin_root + fin_slice:
        cp.wait_send()
    out_a.wait()
    out_q.wait()


def shards(mesh, *args):
    queries, leaf_keys, _, root_keys, _, branch_keys = args[:6]
    T, width = queries.shape
    D = leaf_keys.shape[1]
    H = width // D
    r_rows, b_rows = root_keys.shape[0], branch_keys.shape[0]
    nb, nl = mesh.shape["branch"], mesh.shape["leaf"]
    nc = 2 if nl % 2 == 0 else 1
    nx = nl // nc
    R = T * H
    n_root, n_slice = nb * nl * r_rows, nl * b_rows
    n_keys = n_root + n_slice + T
    any_space = pl.BlockSpec(memory_space=pl.ANY)
    smem = pl.BlockSpec(memory_space=pltpu.SMEM)
    vmem = pl.BlockSpec(memory_space=pltpu.VMEM)
    V = pltpu.VMEM
    dma = pltpu.SemaphoreType.DMA
    np_ = max(nb * nx - 1, 1)
    scratch = [
        V((T, width), f32), V((T, width), f32), V((2, T, D), f32),
        V((nb, nx, nc, 2, r_rows, D), f32), V((nx, nc, 2, b_rows, D), f32),
        V((3, R, D), bf16), V((2, R, D), bf16),
        V((n_keys, 3 * D), bf16), V((n_keys, 2 * D), bf16),
        V((2 * D, n_keys), bf16), V((2 * D, n_keys), bf16),
        V((n_keys, R), f32), V((n_keys, R), f32), V((n_root + n_slice, 2 * D), f32),
        V((T, width), f32), V((T, width), f32),
        V((nb, nx, r_rows, 2 * D), f32), V((nx, b_rows, 2 * D), f32),
        V((nb, nx, r_rows, 2 * D), f32), V((nx, b_rows, 2 * D), f32),
        V((np_, r_rows, 2 * D), f32), V((max(nx - 1, 1), b_rows, 2 * D), f32),
        dma((8,)), dma((2,)), dma((np_,)), dma((np_,)), dma((nx,)), dma((nx,)), dma((2,)), dma((2,)),
        dma((np_,)), dma((np_,)), dma((nx,)), dma((nx,)), dma((2,)), dma((2,)),
    ]
    shape = lambda *s: jax.ShapeDtypeStruct(s, f32)
    return pl.pallas_call(
        functools.partial(kernel, nb, nx, nc, (T, H, D, r_rows, b_rows)),
        out_shape=(
            shape(T, width), shape(T, width), shape(r_rows, 2 * D), shape(b_rows, 2 * D), shape(T, 2 * D),
        ),
        in_specs=[any_space] * 8 + [smem] * 3,
        out_specs=(any_space, any_space, vmem, vmem, vmem),
        scratch_shapes=scratch,
        compiler_params=pltpu.CompilerParams(
            collective_id=0, has_side_effects=True, vmem_limit_bytes=60 * 1024 * 1024
        ),
        name="tree",
    )(*args)


def solution(mesh):
    rows = P(("groups", "branch", "leaf"), None)
    flat = P(("groups", "branch", "leaf"))
    return jax.shard_map(
        functools.partial(shards, mesh),
        mesh=mesh,
        in_specs=(rows,) * 8 + (flat, flat, P(("groups", "branch"))),
        out_specs=(rows,) * 5,
        check_vma=False,
    )
```

time: 189 us -> 32 us (0.17)
  waiting for transfers between devices: 57.9 us -> 0 us
  blocking collectives: 57.2 us -> 0 us
  matrix products: 28.4 us -> 0 us
  Pallas kernels: 0 us -> 24.5 us
  between operations: 14.6 us -> 2.59 us
  other arithmetic: 11.9 us -> 0 us
  local copies, waits for them, and re-layouts: 13.7 us -> 4.64 us
  loops' own time: 4.39 us -> 0 us
    reduce_scatter x3 -> x0, waiting for transfers between devices: 57.2 us -> none  [the longest x1 22.6 us: shards(): lax.psum_scatter(partial_root, 'leaf', scatter_dimension=0, tiled=True)]
    all_gather x4 -> x0, blocking collectives: 57.2 us -> none  [the longest x1 25.1 us: shards(): lax.all_gather(root_keys, ('branch', 'leaf'), axis=0, tiled=True)]
    dot_general x21 -> x0, matrix products: 28.4 us -> none  [the longest x6 6.5 us: masked_scores(): jnp.einsum('thd,kd->thk', query_heads, block_keys, precision=highest)]
    pallas_call x0 -> x1, Pallas kernels: none -> 24.5 us  [shards(): pl.pallas_call(functools.partial(kernel, nb, nx, nc, (T, H, D, r_rows, b_...]
    or x12 -> x0, other arithmetic: 8.83 us -> none  [masked_scores(): visible = in_root | in_slice | in_leaf]
    another operation x2 -> x0, loops' own time: 4.39 us -> none  [the longest x1 2.2 us: shards(): lax.scan(backward_step, jnp.zeros_like(query_heads), (block_ids, all_keys...]
    dynamic_slice x6 -> x0, local copies, waits for them, and re-layouts: 3.51 us -> none  [shards(): lax.scan(forward_step, initial, (block_ids, all_keys, all_values))]
    slice x2 -> x0, local copies, waits for them, and re-layouts: 3.42 us -> none  [the longest x1 1.85 us: shards(): slice_term = pair_rows[root_count:root_count + slice_count]]
  transfers between devices with their start and end apart: 3 -> 0, of which waited for: 3 -> 0; matrix products, arithmetic and copies ran while one was open for 2% -> 0% of each run, Pallas kernels for 0% -> 0%
where the time goes in v1:
time: 32 us; the launch traced here: 31.8 us
  Pallas kernels  24.5 us (77%)
  local copies, waits for them, and re-layouts  4.64 us (14%)
  between operations  2.59 us (8%)
    pallas_call x1, Pallas kernels, shards(): pl.pallas_call(functools.partial(kernel, nb, nx, nc, (T, H, D, r_rows, b_...  24.5 us
    unnamed x13, local copies, waits for them, and re-layouts  4.64 us

profile of v1, /device:TPU:0, one launch (start us, length us, event | category | flops | bytes accessed | tf_op | source)
XLA Modules:
  0.0 31.8 jit_solution(15166771754505900941)
XLA Ops:
  2.6 24.5 %tree.1 = (f32[128,1024]{1,0:T(8,128)}, f32[128,1024]{1,0:T(8,128)}, f32[16,256]{1,0:T(8,128)}, f32[64,256]{1,0:T(8,128)}, f32[128,256]{1,0:T(8,128)}) custom-call(f32[128,1024]{1,0:T(8,128)} %q_hbm.1, f32[128,128]{1,0:T(8,128)} %lk_hbm.1, f32[128,128]{1,0:T(8,128)} %lv_hbm.1, f32[16,128]{1,0:T(8,128)} %rk_hbm.1, f32[16,128]{1,0:T(8,128)} %rv_hbm.1, ...), custom_call_target="tpu_custom_call" | custom-call | tf_op jit(solution)/shard_map/tree/pallas_call | solution.py:350
  27.1 0.0 copy-start
  27.1 1.9 %copy.24 = f32[128,1024]{1,0:T(8,128)} copy(f32[128,1024]{1,0:T(8,128)} %get-tuple-element.10) | data formatting | bytes 1048576
  29.1 0.0 copy-done
  29.1 0.0 copy-start.3
  29.1 0.0 copy-start.2
  29.1 0.8 %copy.25 = f32[128,1024]{1,0:T(8,128)} copy(f32[128,1024]{1,0:T(8,128)S(1)} %copy-done) | data formatting | bytes 1048576
  29.9 0.0 copy-done.3
  29.9 0.0 copy-start.1
  29.9 0.6 %copy.26 = f32[16,256]{1,0:T(8,128)} copy(f32[16,256]{1,0:T(8,128)S(1)} %copy-done.3) | data formatting | bytes 32768
  30.5 0.0 copy-done.2
  30.5 0.6 %copy.27 = f32[64,256]{1,0:T(8,128)} copy(f32[64,256]{1,0:T(8,128)S(1)} %copy-done.2) | data formatting | bytes 131072
  31.1 0.0 copy-done.1
  31.1 0.7 %copy.28 = f32[128,256]{1,0:T(8,128)} copy(f32[128,256]{1,0:T(8,128)S(1)} %copy-done.1) | data formatting | bytes 262144
Async XLA Ops:
  27.1 2.0 %copy-start = (f32[128,1024]{1,0:T(8,128)S(1)}, f32[128,1024]{1,0:T(8,128)}, u32[]{:S(2)}) copy-start(f32[128,1024]{1,0:T(8,128)} %get-tuple-element.11) | copy-start | bytes 1572868
  29.1 0.8 %copy-start.3 = (f32[16,256]{1,0:T(8,128)S(1)}, f32[16,256]{1,0:T(8,128)}, u32[]{:S(2)}) copy-start(f32[16,256]{1,0:T(8,128)} %get-tuple-element.12) | copy-start | bytes 49156
  29.1 1.4 %copy-start.2 = (f32[64,256]{1,0:T(8,128)S(1)}, f32[64,256]{1,0:T(8,128)}, u32[]{:S(2)}) copy-start(f32[64,256]{1,0:T(8,128)} %get-tuple-element.13) | copy-start | bytes 196612
  29.9 1.2 %copy-start.1 = (f32[128,256]{1,0:T(8,128)S(1)}, f32[128,256]{1,0:T(8,128)}, u32[]{:S(2)}) copy-start(f32[128,256]{1,0:T(8,128)} %get-tuple-element.14) | copy-start | bytes 393220

commit v2 on v1

--- a/solution.py
+++ b/solution.py
@@ -39,13 +39,13 @@
 
 def kernel(
     nb, nx, nc, dims,
-    q_hbm, lk_hbm, lv_hbm, rk_hbm, rv_hbm, bk_hbm, bv_hbm, do_hbm, len_ref, par_ref, cut_ref,
-    att_hbm, dq_hbm, droot_ref, dslice_ref, dleaf_ref,
+    q_hbm, lk_hbm, lv_hbm, rk_hbm, rv_hbm, bk_hbm, bv_hbm, do_hbm, len_hbm, par_hbm, cut_hbm,
+    att_ref, dqv_ref, droot_ref, dslice_ref, dleaf_ref,
     q_ref, do_ref, leaf_ref, rootb, sliceb,
     qs, cs, ks, vs, kt, vt, sc, dp, dkv,
-    att_ref, dqv_ref,
+    len_ref, par_ref, cut_ref,
     rc_root, rc_slice, sn_root, sn_slice, rv_root, rv_slice,
-    ld_sem, st_sem, gs_root, gr_root, gs_slice, gr_slice, cs_sem, cr_sem,
+    ld_sem, gs_root, gr_root, gs_slice, gr_slice, cs_sem, cr_sem,
     ss_root, sr_root, ss_slice, sr_slice, es_sem, er_sem,
 ):
     T, H, D, r_rows, b_rows = dims
@@ -81,6 +81,9 @@
         (lv_hbm, leaf_ref.at[1]),
         (q_hbm, q_ref),
         (do_hbm, do_ref),
+        (len_hbm, len_ref),
+        (par_hbm, par_ref),
+        (cut_hbm, cut_ref),
     ]
     loads = [pltpu.make_async_copy(s, d, ld_sem.at[i]) for i, (s, d) in enumerate(loads)]
     for cp in loads:
@@ -290,10 +293,6 @@
         return carry
 
     lax.fori_loop(0, n_pair, outputs, 0)
-    out_a = pltpu.make_async_copy(att_ref, att_hbm, st_sem.at[0])
-    out_q = pltpu.make_async_copy(dqv_ref, dq_hbm, st_sem.at[1])
-    out_a.start()
-    out_q.start()
     dleaf_ref[...] = key_gradients(n_root + n_slice, T)
 
     for cp in fin_slice:
@@ -310,8 +309,15 @@
     droot_ref[...] = total
     for cp in root_sends + slice_sends + core_sends + ex + fin_root + fin_slice:
         cp.wait_send()
-    out_a.wait()
-    out_q.wait()
+
+
+def deliver(*refs):
+    sources, targets, sem = refs[:5], refs[5:10], refs[10]
+    copies = [pltpu.make_async_copy(s, t, sem.at[i]) for i, (s, t) in enumerate(zip(sources, targets))]
+    for cp in copies:
+        cp.start()
+    for cp in copies:
+        cp.wait()
 
 
 def shards(mesh, *args):
@@ -327,9 +333,10 @@
     n_root, n_slice = nb * nl * r_rows, nl * b_rows
     n_keys = n_root + n_slice + T
     any_space = pl.BlockSpec(memory_space=pl.ANY)
-    smem = pl.BlockSpec(memory_space=pltpu.SMEM)
+    hbm = pl.BlockSpec(memory_space=pltpu.HBM)
     vmem = pl.BlockSpec(memory_space=pltpu.VMEM)
     V = pltpu.VMEM
+    S = pltpu.SMEM
     dma = pltpu.SemaphoreType.DMA
     np_ = max(nb * nx - 1, 1)
     scratch = [
@@ -339,27 +346,35 @@
         V((n_keys, 3 * D), bf16), V((n_keys, 2 * D), bf16),
         V((2 * D, n_keys), bf16), V((2 * D, n_keys), bf16),
         V((n_keys, R), f32), V((n_keys, R), f32), V((n_root + n_slice, 2 * D), f32),
-        V((T, width), f32), V((T, width), f32),
+        S((1,), jnp.int32), S((1,), jnp.int32), S((1,), jnp.int32),
         V((nb, nx, r_rows, 2 * D), f32), V((nx, b_rows, 2 * D), f32),
         V((nb, nx, r_rows, 2 * D), f32), V((nx, b_rows, 2 * D), f32),
         V((np_, r_rows, 2 * D), f32), V((max(nx - 1, 1), b_rows, 2 * D), f32),
-        dma((8,)), dma((2,)), dma((np_,)), dma((np_,)), dma((nx,)), dma((nx,)), dma((2,)), dma((2,)),
+        dma((11,)), dma((np_,)), dma((np_,)), dma((nx,)), dma((nx,)), dma((2,)), dma((2,)),
         dma((np_,)), dma((np_,)), dma((nx,)), dma((nx,)), dma((2,)), dma((2,)),
     ]
-    shape = lambda *s: jax.ShapeDtypeStruct(s, f32)
-    return pl.pallas_call(
+    shape = lambda *s: V(s, f32)
+    sizes = ((T, width), (T, width), (r_rows, 2 * D), (b_rows, 2 * D), (T, 2 * D))
+    held = pl.pallas_call(
         functools.partial(kernel, nb, nx, nc, (T, H, D, r_rows, b_rows)),
-        out_shape=(
-            shape(T, width), shape(T, width), shape(r_rows, 2 * D), shape(b_rows, 2 * D), shape(T, 2 * D),
-        ),
-        in_specs=[any_space] * 8 + [smem] * 3,
-        out_specs=(any_space, any_space, vmem, vmem, vmem),
+        out_shape=tuple(shape(*size) for size in sizes),
+        in_specs=[any_space] * 8 + [hbm] * 3,
+        out_specs=(vmem,) * 5,
         scratch_shapes=scratch,
         compiler_params=pltpu.CompilerParams(
             collective_id=0, has_side_effects=True, vmem_limit_bytes=60 * 1024 * 1024
         ),
         name="tree",
     )(*args)
+    return pl.pallas_call(
+        deliver,
+        out_shape=tuple(jax.ShapeDtypeStruct(size, f32) for size in sizes),
+        in_specs=[vmem] * 5,
+        out_specs=(any_space,) * 5,
+        scratch_shapes=[dma((5,))],
+        compiler_params=pltpu.CompilerParams(vmem_limit_bytes=1024 * 1024),
+        name="deliver",
+    )(*held)
 
 
 def solution(mesh):

time: 32 us -> 27.7 us (0.87)
  local copies, waits for them, and re-layouts: 4.64 us -> 0 us
  Pallas kernels: 24.5 us -> 24.9 us
    unnamed x13 -> x0, local copies, waits for them, and re-layouts: 4.64 us -> none
    pallas_call x0 -> x1, Pallas kernels: none -> 1.07 us  [shards(): pl.pallas_call(deliver, out_shape=tuple((jax.ShapeDtypeStruct(size, f32)...]
    pallas_call x1, Pallas kernels: 24.5 us -> 23.8 us  [shards(): pl.pallas_call(functools.partial(kernel, nb, nx, nc, (T, H, D, r_rows, b_...]
where the time goes in v2:
time: 27.7 us; the launch traced here: 27.5 us
  Pallas kernels  24.9 us (90%)
  between operations  2.58 us (9%)
    pallas_call x1, Pallas kernels, shards(): pl.pallas_call(functools.partial(kernel, nb, nx, nc, (T, H, D, r_rows, b_...  23.8 us
    pallas_call x1, Pallas kernels, shards(): pl.pallas_call(deliver, out_shape=tuple((jax.ShapeDtypeStruct(size, f32)...  1.07 us

profile of v2, /device:TPU:0, one launch (start us, length us, event | category | flops | bytes accessed | tf_op | source)
XLA Modules:
  0.0 27.5 jit_solution(16180610080749319062)
XLA Ops:
  2.6 23.8 %tree.1 = (f32[128,1024]{1,0:T(8,128)S(1)}, f32[128,1024]{1,0:T(8,128)S(1)}, f32[16,256]{1,0:T(8,128)S(1)}, f32[64,256]{1,0:T(8,128)S(1)}, f32[128,256]{1,0:T(8,128)S(1)}) custom-call(f32[128,1024]{1,0:T(8,128)} %q_hbm.1, f32[128,128]{1,0:T(8,128)} %lk_hbm.1, f32[128,128]{1,0:T(8,128)} %lv_hbm.1, f32[16,128]{1,0:T(8,128)} %rk_hbm.1, f32[16,128]{1,0:T(8,128)} %rv_hbm.1, ...), custom_call_target="tpu_custom_call" | custom-call | tf_op jit(solution)/shard_map/tree/pallas_call | solution.py:358
  26.4 1.1 %deliver.1 = (f32[128,1024]{1,0:T(8,128)}, f32[128,1024]{1,0:T(8,128)}, f32[16,256]{1,0:T(8,128)}, f32[64,256]{1,0:T(8,128)}, f32[128,256]{1,0:T(8,128)}) custom-call(f32[128,1024]{1,0:T(8,128)S(1)} %get-tuple-element.10.refs_0_, f32[128,1024]{1,0:T(8,128)S(1)} %get-tuple-element.11.refs_1_, f32[16,256]{1,0:T(8,128)S(1)} %get-tuple-element.12.refs_2_, ...), custom_call_target="tpu_custom_call" | custom-call | tf_op jit(solution)/shard_map/deliver/pallas_call | solution.py:369

commit v3 on v2

--- a/solution.py
+++ b/solution.py
@@ -239,20 +239,22 @@
         v = mm(w1, c12) + mm(w2, c12)
         return side(a[:, :D] + a[:, D:], v[:, :D] + v[:, D:])
 
+    block = 2 * chunk if n_root % (2 * chunk) == 0 and n_slice % (2 * chunk) == 0 else chunk
+
     def gradient_block(i, carry):
-        at = pl.multiple_of(i * chunk, chunk)
-        dkv[pl.ds(at, chunk), :] = key_gradients(at, chunk)
+        at = pl.multiple_of(i * block, block)
+        dkv[pl.ds(at, block), :] = key_gradients(at, block)
         return carry
 
     root_g = dkv.at[:n_root].reshape(nb, nx, nc, r_rows, 2 * D)
     slice_g = dkv.at[n_root : n_root + n_slice].reshape(nx, nc, b_rows, 2 * D)
-    lax.fori_loop(0, n_root // chunk, gradient_block, 0)
+    lax.fori_loop(0, n_root // block, gradient_block, 0)
     ex = []
     if nc == 2:
         cp = remote(root_g.at[:, :, other], rc_root, es_sem.at[0], er_sem.at[0], dev(b, x, other))
         cp.start()
         ex.append(cp)
-    lax.fori_loop(n_root // chunk, (n_root + n_slice) // chunk, gradient_block, 0)
+    lax.fori_loop(n_root // block, (n_root + n_slice) // block, gradient_block, 0)
     if nc == 2:
         cp = remote(slice_g.at[:, other], rc_slice, es_sem.at[1], er_sem.at[1], dev(b, x, other))
         cp.start()

time: 27.7 us -> 27.3 us (0.986)
  Pallas kernels: 24.9 us -> 24.6 us
    pallas_call x1, Pallas kernels: 23.8 us -> 23.5 us  [shards(): pl.pallas_call(functools.partial(kernel, nb, nx, nc, (T, H, D, r_rows, b_...]
where the time goes in v3:
time: 27.3 us; the launch traced here: 27.2 us
  Pallas kernels  24.6 us (90%)
  between operations  2.58 us (9%)
    pallas_call x1, Pallas kernels, shards(): pl.pallas_call(functools.partial(kernel, nb, nx, nc, (T, H, D, r_rows, b_...  23.5 us
    pallas_call x1, Pallas kernels, shards(): pl.pallas_call(deliver, out_shape=tuple((jax.ShapeDtypeStruct(size, f32)...  1.07 us

profile of v3, /device:TPU:0, one launch (start us, length us, event | category | flops | bytes accessed | tf_op | source)
XLA Modules:
  0.0 27.2 jit_solution(4323116606627559640)
XLA Ops:
  2.6 23.5 %tree.1 = (f32[128,1024]{1,0:T(8,128)S(1)}, f32[128,1024]{1,0:T(8,128)S(1)}, f32[16,256]{1,0:T(8,128)S(1)}, f32[64,256]{1,0:T(8,128)S(1)}, f32[128,256]{1,0:T(8,128)S(1)}) custom-call(f32[128,1024]{1,0:T(8,128)} %q_hbm.1, f32[128,128]{1,0:T(8,128)} %lk_hbm.1, f32[128,128]{1,0:T(8,128)} %lv_hbm.1, f32[16,128]{1,0:T(8,128)} %rk_hbm.1, f32[16,128]{1,0:T(8,128)} %rv_hbm.1, ...), custom_call_target="tpu_custom_call" | custom-call | tf_op jit(solution)/shard_map/tree/pallas_call | solution.py:360
  26.1 1.1 %deliver.1 = (f32[128,1024]{1,0:T(8,128)}, f32[128,1024]{1,0:T(8,128)}, f32[16,256]{1,0:T(8,128)}, f32[64,256]{1,0:T(8,128)}, f32[128,256]{1,0:T(8,128)}) custom-call(f32[128,1024]{1,0:T(8,128)S(1)} %get-tuple-element.10.refs_0_, f32[128,1024]{1,0:T(8,128)S(1)} %get-tuple-element.11.refs_1_, f32[16,256]{1,0:T(8,128)S(1)} %get-tuple-element.12.refs_2_, ...), custom_call_target="tpu_custom_call" | custom-call | tf_op jit(solution)/shard_map/deliver/pallas_call | solution.py:371
